TPU v7x, 32 devices: a whole 2x2x4 slice. The times are simulated.
32 devices in a mesh: gx: 4 (over y, x), gy: 2 (over core), gz: 4 (over z).
Axes of the slice: x: 2, y: 2, z: 4, core: 2. Of those that a mesh axis runs over, the one named last changes fastest.
Arguments:
- initial: float32 [256, 64, 1024], P('gx', 'gy', 'gz'), may hold values from -6 to 6
- right_side: float32 [256, 64, 1024], P('gx', 'gy', 'gz'), may hold values from -12 to 12
- shift_field: float32 [256, 64, 1024], P('gx', 'gy', 'gz'), may hold values from 0.5 to 8
Outputs:
- relaxed: float32 [256, 64, 1024], P('gx', 'gy', 'gz')
All inputs are finite; a program needn't handle non-finite values.
Results may differ from a plain program's by a relative error of at most 0.00002.
Values sent between devices are 32-bit elements; how exact they have to be, the bound alone decides.
A program may use at most 128 MiB of HBM per device.

v0:
```python
import functools

import jax
import jax.numpy as jnp
import numpy as np
from jax import lax
from jax.experimental import pallas as pl
from jax.experimental.pallas import tpu as pltpu
from jax.sharding import PartitionSpec as P

SWEEPS = 4
WEIGHT = np.float32(0.8)
KEEP = np.float32(1.0) - WEIGHT
AXES = ("gx", "gy", "gz")
MESH = pl.DeviceIdType.MESH
ROWS = 8
LANES = 128


def beside(axis, step):
    count = lax.axis_size(axis)
    return {axis: lax.rem(lax.axis_index(axis) + (count + step), count)}


def iota(dim, shape):
    return lax.broadcasted_iota(jnp.int32, shape, dim)


def turned(block, shift, dim):
    size = block.shape[dim]
    shift = shift % size
    return block if shift == 0 else pltpu.roll(block, shift, dim)


def kernel(init_ref, rhs_ref, shift_ref, out_ref, v, q, w, ys, yh, zs, zh, zp, wz, load, send, recv):
    nx, ny, nz = out_ref.shape
    groups, bands, tiles = nx // ROWS, ny // ROWS, nz // LANES

    barrier = pltpu.get_barrier_semaphore()
    for axis in AXES:
        for step in (-1, 1):
            pl.semaphore_signal(barrier, inc=1, device_id=beside(axis, step), device_id_type=MESH)

    def init_copy(g):
        return pltpu.make_async_copy(
            init_ref.at[pl.ds(g * ROWS, ROWS)], v.at[0, pl.ds(g * ROWS + 1, ROWS)], load.at[g]
        )

    for g in range(groups):
        init_copy(g).start()
    rhs_copy = pltpu.make_async_copy(rhs_ref, q, load.at[groups])
    shift_copy = pltpu.make_async_copy(shift_ref, w, load.at[groups + 1])
    rhs_copy.start()
    shift_copy.start()

    def remote(src, dst, t, face, axis, step):
        return pltpu.make_async_remote_copy(
            src_ref=src,
            dst_ref=dst,
            send_sem=send.at[t, face],
            recv_sem=recv.at[t, face],
            device_id=beside(axis, step),
            device_id_type=MESH,
        )

    def x_copies(t):
        low = init_ref.at[0] if t == 0 else v.at[t, 1]
        high = init_ref.at[nx - 1] if t == 0 else v.at[t, nx]
        return (
            remote(high, v.at[t, 0], t, 0, "gx", 1),
            remote(low, v.at[t, nx + 1], t, 1, "gx", -1),
        )

    def z_copies(t):
        return (
            remote(zs.at[t, 1], zh.at[t, 0], t, 4, "gz", 1),
            remote(zs.at[t, 0], zh.at[t, 1], t, 5, "gz", -1),
        )

    def y_copies(t):
        return (
            remote(ys.at[t, 1], yh.at[t, 0], t, 2, "gy", 1),
            remote(ys.at[t, 0], yh.at[t, 1], t, 3, "gy", -1),
        )

    row = iota(0, (ROWS, nz))
    row1 = iota(0, (ROWS, LANES))
    lane = iota(1, (ny, LANES))
    lane1 = iota(1, (ROWS, LANES))

    def put(t, x, new):
        if t < SWEEPS:
            v[t, x + 1] = new
        else:
            out_ref[x] = new

    def get(t, x):
        return v[t, x + 1] if t < SWEEPS else out_ref[x]

    def pack_rows(t, g, planes):
        low, high = jnp.zeros((2, ROWS, nz), jnp.float32)
        for j, new in enumerate(planes):
            low = jnp.where(row == j, turned(new[:ROWS], j, 0), low)
            high = jnp.where(row == j, turned(new[ny - ROWS :], j + 1, 0), high)
        ys[t, 0, pl.ds(pl.multiple_of(g * ROWS, ROWS), ROWS)] = low
        ys[t, 1, pl.ds(pl.multiple_of(g * ROWS, ROWS), ROWS)] = high

    def pack_columns(g, planes, carry):
        low, high = jnp.zeros((2, ny, LANES), jnp.float32)
        for j, new in enumerate(planes):
            low = jnp.where(lane == j, turned(new[:, :LANES], j, 1), low)
            high = jnp.where(lane == j, turned(new[:, nz - LANES :], j + 1, 1), high)
        return carry[0] + pltpu.roll(low, g * ROWS, 1), carry[1] + pltpu.roll(high, g * ROWS, 1)

    def start(copies):
        for copy in copies:
            copy.start()

    def wait(copies):
        for copy in copies:
            copy.wait()

    blank = (jnp.zeros((ny, LANES), jnp.float32), jnp.zeros((ny, LANES), jnp.float32))

    pl.semaphore_wait(barrier, 2 * len(AXES))
    start(x_copies(0))

    def first_pack(g, carry):
        init_copy(g).wait()
        planes = [v[0, g * ROWS + 1 + j] for j in range(ROWS)]
        pack_rows(0, g, planes)
        return pack_columns(g, planes, carry)

    packed = lax.fori_loop(0, groups, first_pack, blank)
    zs[0, 0], zs[0, 1] = packed
    start(z_copies(0) + y_copies(0))

    rhs_copy.wait()
    shift_copy.wait()

    def prepare(g, carry):
        planes = []
        for j in range(ROWS):
            x = g * ROWS + j
            ratio = WEIGHT / (6.0 + w[x])
            w[x] = ratio
            q[x] = ratio * q[x]
            planes.append(ratio)
        return pack_columns(g, planes, carry)

    packed = lax.fori_loop(0, groups, prepare, blank)
    wz[0], wz[1] = packed

    def blend(t, x, k, y_low, y_high, z_low, z_high):
        at = slice(ROWS * k, ROWS * k + ROWS)
        c = v[t, x + 1, at]
        total = v[t, x, at] + v[t, x + 2, at]
        above = v[t, x + 1, ROWS * k - ROWS : ROWS * k] if k else None
        below = v[t, x + 1, ROWS * k + ROWS : ROWS * k + 2 * ROWS] if k + 1 < bands else None
        above = turned(above, 1, 0) if k else y_low
        below = turned(below, -1, 0) if k + 1 < bands else y_high
        total = total + jnp.where(row == 0, above, turned(c, 1, 0))
        total = total + jnp.where(row == ROWS - 1, below, turned(c, -1, 0))
        before = [turned(c[:, LANES * i : LANES * i + LANES], 1, 1) for i in range(tiles)]
        after = [turned(c[:, LANES * i : LANES * i + LANES], -1, 1) for i in range(tiles)]
        before_edge = [z_low] + before[:-1]
        after_edge = after[1:] + [z_high]
        total = total + jnp.concatenate(
            [
                jnp.where(lane1 == 0, before_edge[i], before[i])
                + jnp.where(lane1 == LANES - 1, after_edge[i], after[i])
                for i in range(tiles)
            ],
            axis=1,
        )
        return (KEEP * c + q[x, at]) + w[x, at] * total

    def bulk_group(t, ks, g, carry, first=0, last=ROWS):
        base = g * ROWS
        aligned = pl.multiple_of(base, ROWS)
        y_low = yh[t, 0, pl.ds(aligned, ROWS)] if 0 in ks else None
        y_high = yh[t, 1, pl.ds(aligned, ROWS)] if bands - 1 in ks else None
        none = jnp.zeros((ROWS, LANES), jnp.float32)
        low = [none for _ in ks]
        high = [none for _ in ks]
        for j in range(first, last):
            x = base + j
            for i, k in enumerate(ks):
                new = blend(
                    t,
                    x,
                    k,
                    turned(y_low, -j, 0) if k == 0 else None,
                    turned(y_high, ROWS - 1 - j, 0) if k == bands - 1 else None,
                    none,
                    none,
                )
                if t + 1 < SWEEPS:
                    v[t + 1, x + 1, ROWS * k : ROWS * k + ROWS] = new
                else:
                    out_ref[x, ROWS * k : ROWS * k + ROWS] = new
                low[i] = jnp.where(lane1 == j, turned(new[:, :LANES], j, 1), low[i])
                high[i] = jnp.where(lane1 == j, turned(new[:, nz - LANES :], j + 1, 1), high[i])
        return tuple(
            old + pltpu.roll(add, base, 1) for old, add in zip(carry, low + high)
        )

    def bulk(t, ks):
        none = jnp.zeros((ROWS, LANES), jnp.float32)
        carry = bulk_group(t, ks, 0, (none,) * (2 * len(ks)), first=1)
        carry = lax.fori_loop(1, groups - 1, functools.partial(bulk_group, t, ks), carry)
        carry = bulk_group(t, ks, groups - 1, carry, last=ROWS - 1)
        for i, k in enumerate(ks):
            zp[0, ROWS * k : ROWS * k + ROWS] = carry[i]
            zp[1, ROWS * k : ROWS * k + ROWS] = carry[len(ks) + i]

    def edge_plane(t, x):
        base = x // ROWS * ROWS
        j = x - base
        parts = []
        for k in range(bands):
            at = slice(ROWS * k, ROWS * k + ROWS)
            parts.append(
                blend(
                    t,
                    x,
                    k,
                    turned(yh[t, 0, base : base + ROWS], -j, 0),
                    turned(yh[t, 1, base : base + ROWS], ROWS - 1 - j, 0),
                    turned(zh[t, 0, at], -x, 1),
                    turned(zh[t, 1, at], LANES - 1 - x, 1),
                )
            )
        return jnp.concatenate(parts, axis=0)

    def mend_group(t, g, carry, first=0, last=ROWS):
        base = g * ROWS
        back = lax.rem(LANES - base, LANES)
        z_low = pltpu.roll(zs[t, 0], back, 1)
        z_high = pltpu.roll(zs[t, 1], back, 1)
        planes = []
        for j in range(ROWS):
            plane = get(t, base + j)
            if first <= j < last:
                parts = [plane[:, LANES * i : LANES * i + LANES] for i in range(tiles)]
                parts[0] = jnp.where(lane == 0, turned(z_low, -j, 1), parts[0])
                parts[-1] = jnp.where(lane == LANES - 1, turned(z_high, LANES - 1 - j, 1), parts[-1])
                plane = jnp.concatenate(parts, axis=1)
                put(t, base + j, plane)
            planes.append(plane)
        if t < SWEEPS:
            pack_rows(t, g, planes)
        return carry

    outer = tuple(sorted({0, bands - 1}))
    inner = tuple(range(1, bands - 1))
    for t in range(SWEEPS):
        if inner:
            bulk(t, inner)
        wait(y_copies(t))
        bulk(t, outer)
        wait(x_copies(t) + z_copies(t))
        first_plane, last_plane = edge_plane(t, 0), edge_plane(t, nx - 1)
        put(t + 1, 0, first_plane)
        put(t + 1, nx - 1, last_plane)
        if t + 1 < SWEEPS:
            start(x_copies(t + 1))
        for side, cut, turn in ((0, slice(0, LANES), 0), (1, slice(nz - LANES, nz), 1)):
            face = zp[side] + wz[side] * zh[t, side]
            face = jnp.where(lane == 0, turned(first_plane[:, cut], turn, 1), face)
            face = jnp.where(lane == nx - 1, turned(last_plane[:, cut], nx - 1 + turn, 1), face)
            zs[t + 1, side] = face
        if t + 1 < SWEEPS:
            start(z_copies(t + 1))
        mend_group(t + 1, 0, 0, first=1)
        lax.fori_loop(1, groups - 1, functools.partial(mend_group, t + 1), 0)
        mend_group(t + 1, groups - 1, 0, last=ROWS - 1)
        if t + 1 < SWEEPS:
            start(y_copies(t + 1))


def shards(initial, right_side, shift_field):
    nx, ny, nz = initial.shape
    assert nx % ROWS == 0 and 2 * ROWS <= nx <= LANES
    assert ny % ROWS == 0 and nz % LANES == 0
    faces = 2 * len(AXES)
    return pl.pallas_call(
        kernel,
        out_shape=pltpu.VMEM((nx, ny, nz), jnp.float32),
        in_specs=[pl.BlockSpec(memory_space=pltpu.HBM)] * 3,
        out_specs=pl.BlockSpec(memory_space=pltpu.VMEM),
        scratch_shapes=[
            pltpu.VMEM((SWEEPS, nx + 2, ny, nz), jnp.float32),
            pltpu.VMEM((nx, ny, nz), jnp.float32),
            pltpu.VMEM((nx, ny, nz), jnp.float32),
            pltpu.VMEM((SWEEPS, 2, nx, nz), jnp.float32),
            pltpu.VMEM((SWEEPS, 2, nx, nz), jnp.float32),
            pltpu.VMEM((SWEEPS + 1, 2, ny, LANES), jnp.float32),
            pltpu.VMEM((SWEEPS, 2, ny, LANES), jnp.float32),
            pltpu.VMEM((2, ny, LANES), jnp.float32),
            pltpu.VMEM((2, ny, LANES), jnp.float32),
            pltpu.SemaphoreType.DMA((nx // ROWS + 2,)),
            pltpu.SemaphoreType.DMA((SWEEPS, faces)),
            pltpu.SemaphoreType.DMA((SWEEPS, faces)),
        ],
        compiler_params=pltpu.CompilerParams(
            collective_id=0, has_side_effects=True, vmem_limit_bytes=32 * 1024 * 1024
        ),
    )(*(pltpu.with_memory_space_constraint(a, pltpu.HBM) for a in (initial, right_side, shift_field)))


def solution(mesh):
    spec = P(*AXES)
    return jax.shard_map(
        shards, mesh=mesh, in_specs=(spec, spec, spec), out_specs=spec, check_vma=False
    )
```

profile of v0, /device:TPU:0, one launch (start us, length us, event | category | flops | bytes accessed | tf_op | source)
XLA Modules:
  0.0 34.0 jit_solution(17670956541122752608)
XLA Ops:
  0.0 32.7 %shard_map.37 = f32[64,32,256]{2,1,0:T(8,128)S(1)} custom-call(f32[64,32,256]{2,1,0:T(8,128)} %init_ref.1, f32[64,32,256]{2,1,0:T(8,128)} %rhs_ref.1, f32[64,32,256]{2,1,0:T(8,128)} %shift_ref.1), custom_call_target="tpu_custom_call" | custom-call | tf_op jit(solution)/shard_map/pallas_call | solution.py:287
  32.7 1.3 %copy.5 = f32[64,32,256]{2,1,0:T(8,128)} copy(f32[64,32,256]{2,1,0:T(8,128)S(1)} %shard_map.37) | data formatting | bytes 4194304
where the time goes:
time: 34.2 us; the launch traced here: 34 us
  Pallas kernels  32.7 us (96%)
  local copies, waits for them, and re-layouts  1.32 us (4%)
    pallas_call x1, Pallas kernels, shards(): pl.pallas_call(kernel, out_shape=pltpu.VMEM((nx, ny, nz), jnp.float32), i...  32.7 us
    unnamed x1, local copies, waits for them, and re-layouts  1.32 us

commit v1 on v0

v1 whole, which is shorter than its diff:
```python
import functools

import jax
import jax.numpy as jnp
import numpy as np
from jax import lax
from jax.experimental import pallas as pl
from jax.experimental.pallas import tpu as pltpu
from jax.sharding import PartitionSpec as P

SWEEPS = 4
WEIGHT = np.float32(0.8)
KEEP = np.float32(1.0) - WEIGHT
AXES = ("gx", "gy", "gz")
MESH = pl.DeviceIdType.MESH
ROWS = 8
LANES = 128
GROUP = 16
PREPARED = 8
CHUNKS = 4


def beside(axis, step):
    count = lax.axis_size(axis)
    return {axis: lax.rem(lax.axis_index(axis) + (count + step), count)}


def iota(dim, shape):
    return lax.broadcasted_iota(jnp.int32, shape, dim)


def turned(block, shift, dim):
    size = block.shape[dim]
    shift = shift % size
    return block if shift == 0 else pltpu.roll(block, shift, dim)


def kernel(init_ref, rhs_ref, shift_ref, out_ref, v, q, w, z, zh, load, send, recv):
    nx, ny, nz = out_ref.shape
    groups, bands, tiles = nx // GROUP, ny // ROWS, nz // LANES
    per = nx // CHUNKS

    barrier = pltpu.get_barrier_semaphore()
    for axis in AXES:
        for step in (-1, 1):
            pl.semaphore_signal(barrier, inc=1, device_id=beside(axis, step), device_id_type=MESH)

    def part(array, j):
        return array.at[:, :, pl.ds(LANES * j, LANES)]

    def init_copies(c):
        return [
            pltpu.make_async_copy(
                init_ref.at[pl.ds(c * per, per), :, pl.ds(LANES * j, LANES)],
                v.at[0, pl.ds(c * per + 1, per), j, pl.ds(ROWS, ny)],
                load.at[c * tiles + j],
            )
            for j in range(tiles)
        ]

    def field_copies(array, held, slot):
        return [
            pltpu.make_async_copy(part(array, j), held.at[:, j], load.at[(CHUNKS + slot) * tiles + j])
            for j in range(tiles)
        ]

    def start(copies):
        for copy in copies:
            copy.start()

    def wait(copies):
        for copy in copies:
            copy.wait()

    for c in range(CHUNKS):
        start(init_copies(c))
    field_loads = field_copies(shift_ref, w, 0) + field_copies(rhs_ref, q, 1)
    start(field_loads)

    def remote(src, dst, t, face, axis, step):
        return pltpu.make_async_remote_copy(
            src_ref=src,
            dst_ref=dst,
            send_sem=send.at[t, face],
            recv_sem=recv.at[t, face],
            device_id=beside(axis, step),
            device_id_type=MESH,
        )

    def x_copies(t):
        def plane(x):
            return v.at[t, x + 1, :, pl.ds(ROWS, ny)]

        return (
            remote(plane(nx - 1), plane(-1), t, 0, "gx", 1),
            remote(plane(0), plane(nx), t, 1, "gx", -1),
        )

    def y_copies(t):
        def row(y):
            return v.at[t, pl.ds(1, nx), :, pl.ds(ROWS + y, 1)]

        return (
            remote(row(ny - 1), row(-1), t, 2, "gy", 1),
            remote(row(0), row(ny), t, 3, "gy", -1),
        )

    def z_copies(t):
        return (
            remote(z.at[t], zh.at[t, 0], t, 4, "gz", 1),
            remote(z.at[t], zh.at[t, 1], t, 5, "gz", -1),
        )

    lane = iota(1, (ROWS, LANES))
    first_lane = lane == 0
    last_lane = lane == LANES - 1
    blank = jnp.zeros((ROWS, LANES), jnp.float32)

    def rows(k, shift=0):
        return slice(ROWS + ROWS * k + shift, 2 * ROWS + ROWS * k + shift)

    def spots(x):
        return (lane == 2 * x % LANES) | (lane == (2 * x - 1) % LANES)

    def ends(low, high):
        return jnp.where(first_lane, low, high)

    def packed(held, x, low, high):
        return jnp.where(spots(x), turned(ends(low, high), 2 * x, 1), held)

    def put(t, x, j, k, new):
        if t < SWEEPS:
            v[t, x + 1, j, rows(k)] = new
        else:
            out_ref[x, ROWS * k : ROWS * k + ROWS, LANES * j : LANES * j + LANES] = new

    def get(t, x, j, k):
        if t < SWEEPS:
            return v[t, x + 1, j, rows(k)]
        return out_ref[x, ROWS * k : ROWS * k + ROWS, LANES * j : LANES * j + LANES]

    def put_lane(t, x, j, k, new, mask):
        if t < SWEEPS:
            pltpu.store(v.at[t, x + 1, j, pl.ds(ROWS + ROWS * k, ROWS)], new, mask=mask)
        else:
            pltpu.store(
                out_ref.at[x, pl.ds(ROWS * k, ROWS), pl.ds(LANES * j, LANES)], new, mask=mask
            )

    def packed_all(low, high, planes=None):
        held = [blank] * bands
        for x in range(nx) if planes is None else planes:
            for k in range(bands):
                held[k] = packed(held[k], x, low(x, k), high(x, k))
        return held

    for c in range(CHUNKS):
        wait(init_copies(c))
    face = packed_all(lambda x, k: v[0, x + 1, 0, rows(k)], lambda x, k: v[0, x + 1, tiles - 1, rows(k)])
    for k in range(bands):
        z[0, ROWS * k : ROWS * k + ROWS] = face[k]

    pl.semaphore_wait(barrier, 2 * len(AXES))
    start(z_copies(0) + x_copies(0) + y_copies(0))

    wait(field_loads)

    def prepare(g, carry):
        for i in range(PREPARED):
            x = g * PREPARED + i
            for k in range(bands):
                at = slice(ROWS * k, ROWS * k + ROWS)
                for j in range(tiles):
                    ratio = WEIGHT / (6.0 + w[x, j, at])
                    w[x, j, at] = ratio
                    q[x, j, at] = ratio * q[x, j, at]
        return carry

    lax.fori_loop(0, nx // PREPARED, prepare, 0)
    wz = packed_all(
        lambda x, k: w[x, 0, ROWS * k : ROWS * k + ROWS], lambda x, k: w[x, tiles - 1, ROWS * k : ROWS * k + ROWS]
    )

    def bulk_group(t, g, carry):
        base = g * GROUP
        seen = {}

        def plane(i):
            if i not in seen:
                x = base + i
                if i < 0:
                    x = jnp.maximum(x, 0)
                if i == GROUP:
                    x = jnp.minimum(x, nx - 1)
                seen[i] = [[v[t, x + 1, j, rows(k)] for k in range(bands)] for j in range(tiles)]
                if i < 0:
                    inside = jnp.where(g > 0, 1.0, 0.0)
                    seen[i] = [[inside * cell for cell in column] for column in seen[i]]
                if i == GROUP:
                    inside = jnp.where(g < groups - 1, 1.0, 0.0)
                    seen[i] = [[inside * cell for cell in column] for column in seen[i]]
            return seen[i]

        for i in range(GROUP):
            x = base + i
            centre, below, above = plane(i), plane(i - 1), plane(i + 1)
            for k in range(bands):
                at = slice(ROWS * k, ROWS * k + ROWS)
                before = [turned(centre[j][k], 1, 1) for j in range(tiles)]
                after = [turned(centre[j][k], -1, 1) for j in range(tiles)]
                for j in range(tiles):
                    total = v[t, x + 1, j, rows(k, -1)] + v[t, x + 1, j, rows(k, 1)]
                    total = total + (below[j][k] + above[j][k])
                    low = before[j - 1] if j else 0.0
                    high = after[j + 1] if j + 1 < tiles else 0.0
                    total = total + (
                        jnp.where(first_lane, low, before[j]) + jnp.where(last_lane, high, after[j])
                    )
                    put(t + 1, x, j, k, (KEEP * centre[j][k] + q[x, j, at]) + w[x, j, at] * total)
        return carry

    def bulk(t):
        lax.fori_loop(0, groups, functools.partial(bulk_group, t), 0)

    def mend(t, faces):
        for x in range(1, nx - 1):
            for k in range(bands):
                value = turned(faces[k], -2 * x, 1)
                put_lane(t, x, 0, k, value, first_lane)
                put_lane(t, x, tiles - 1, k, value, last_lane)

    even = lane % 2 == 0
    edges = ((0, -1), (nx - 1, nx))
    for t in range(SWEEPS):
        wait(y_copies(t))
        bulk(t)
        partial = packed_all(
            lambda x, k: get(t + 1, x, 0, k), lambda x, k: get(t + 1, x, tiles - 1, k), range(1, nx - 1)
        )
        wait(x_copies(t) + z_copies(t))
        planes = []
        for x, outside in edges:
            plane = [
                [
                    get(t + 1, x, j, k)
                    + w[x, j, ROWS * k : ROWS * k + ROWS] * v[t, outside + 1, j, rows(k)]
                    for k in range(bands)
                ]
                for j in range(tiles)
            ]
            for k in range(bands):
                partial[k] = packed(partial[k], x, plane[0][k], plane[-1][k])
            planes.append(plane)
        faces = []
        for k in range(bands):
            at = slice(ROWS * k, ROWS * k + ROWS)
            halo = jnp.where(even, turned(zh[t, 0, at], 1, 1), turned(zh[t, 1, at], -1, 1))
            faces.append(partial[k] + wz[k] * halo)
            if t + 1 < SWEEPS:
                z[t + 1, at] = faces[k]
        if t + 1 < SWEEPS:
            start(z_copies(t + 1))
        for (x, _), plane in zip(edges, planes):
            for k in range(bands):
                value = turned(faces[k], -2 * x, 1)
                plane[0][k] = jnp.where(first_lane, value, plane[0][k])
                plane[-1][k] = jnp.where(last_lane, value, plane[-1][k])
                for j in range(tiles):
                    put(t + 1, x, j, k, plane[j][k])
        if t + 1 < SWEEPS:
            start(x_copies(t + 1))
        mend(t + 1, faces)
        if t + 1 < SWEEPS:
            start(y_copies(t + 1))


def shards(initial, right_side, shift_field):
    nx, ny, nz = initial.shape
    assert nx % GROUP == 0 and nx % PREPARED == 0 and nx % CHUNKS == 0 and 2 * nx <= LANES
    assert ny % ROWS == 0 and nz % LANES == 0
    faces, tiles = 2 * len(AXES), nz // LANES
    return pl.pallas_call(
        kernel,
        out_shape=pltpu.VMEM((nx, ny, nz), jnp.float32),
        in_specs=[pl.BlockSpec(memory_space=pltpu.HBM)] * 3,
        out_specs=pl.BlockSpec(memory_space=pltpu.VMEM),
        scratch_shapes=[
            pltpu.VMEM((SWEEPS, nx + 2, tiles, ny + 2 * ROWS, LANES), jnp.float32),
            pltpu.VMEM((nx, tiles, ny, LANES), jnp.float32),
            pltpu.VMEM((nx, tiles, ny, LANES), jnp.float32),
            pltpu.VMEM((SWEEPS, ny, LANES), jnp.float32),
            pltpu.VMEM((SWEEPS, 2, ny, LANES), jnp.float32),
            pltpu.SemaphoreType.DMA(((CHUNKS + 2) * tiles,)),
            pltpu.SemaphoreType.DMA((SWEEPS, faces)),
            pltpu.SemaphoreType.DMA((SWEEPS, faces)),
        ],
        compiler_params=pltpu.CompilerParams(
            collective_id=0, has_side_effects=True, vmem_limit_bytes=40 * 1024 * 1024
        ),
    )(*(pltpu.with_memory_space_constraint(a, pltpu.HBM) for a in (initial, right_side, shift_field)))


def solution(mesh):
    spec = P(*AXES)
    return jax.shard_map(
        shards, mesh=mesh, in_specs=(spec, spec, spec), out_specs=spec, check_vma=False
    )
```

time: 34.2 us -> 23.2 us (0.68)
  Pallas kernels: 32.7 us -> 21.7 us
    pallas_call x1, Pallas kernels: 32.7 us -> 21.7 us  [shards(): pl.pallas_call(kernel, out_shape=pltpu.VMEM((nx, ny, nz), jnp.float32), i...]
where the time goes in v1:
time: 23.2 us; the launch traced here: 23.1 us
  Pallas kernels  21.7 us (94%)
  local copies, waits for them, and re-layouts  1.32 us (6%)
    pallas_call x1, Pallas kernels, shards(): pl.pallas_call(kernel, out_shape=pltpu.VMEM((nx, ny, nz), jnp.float32), i...  21.7 us
    unnamed x1, local copies, waits for them, and re-layouts  1.32 us

profile of v1, /device:TPU:0, one launch (start us, length us, event | category | flops | bytes accessed | tf_op | source)
XLA Modules:
  0.0 23.1 jit_solution(13303544326529188882)
XLA Ops:
  0.0 21.7 %shard_map.37 = f32[64,32,256]{2,1,0:T(8,128)S(1)} custom-call(f32[64,32,256]{2,1,0:T(8,128)} %init_ref.1, f32[64,32,256]{2,1,0:T(8,128)} %rhs_ref.1, f32[64,32,256]{2,1,0:T(8,128)} %shift_ref.1), custom_call_target="tpu_custom_call" | custom-call | tf_op jit(solution)/shard_map/pallas_call | solution.py:282
  21.7 1.3 %copy.5 = f32[64,32,256]{2,1,0:T(8,128)} copy(f32[64,32,256]{2,1,0:T(8,128)S(1)} %shard_map.37) | data formatting | bytes 4194304

commit v2 on v1

--- a/solution.py
+++ b/solution.py
@@ -107,8 +107,8 @@
 
     def z_copies(t):
         return (
-            remote(z.at[t], zh.at[t, 0], t, 4, "gz", 1),
-            remote(z.at[t], zh.at[t, 1], t, 5, "gz", -1),
+            remote(z.at[t, 1], zh.at[t, 0], t, 4, "gz", 1),
+            remote(z.at[t, 0], zh.at[t, 1], t, 5, "gz", -1),
         )
 
     lane = iota(1, (ROWS, LANES))
@@ -119,14 +119,20 @@
     def rows(k, shift=0):
         return slice(ROWS + ROWS * k + shift, 2 * ROWS + ROWS * k + shift)
 
-    def spots(x):
-        return (lane == 2 * x % LANES) | (lane == (2 * x - 1) % LANES)
-
-    def ends(low, high):
-        return jnp.where(first_lane, low, high)
-
-    def packed(held, x, low, high):
-        return jnp.where(spots(x), turned(ends(low, high), 2 * x, 1), held)
+    def spots(x, k):
+        return (lane == (2 * x + k % 2) % LANES) | (lane == (2 * x + k % 2 - 1) % LANES)
+
+    def packed(held, x, k, low, high):
+        ends = jnp.where(first_lane, low, high)
+        return jnp.where(spots(x, k), turned(ends, 2 * x + k % 2, 1), held)
+
+    even = lane % 2 == 0
+
+    def ship(t, faces):
+        for m in range(bands // 2):
+            at = slice(ROWS * m, ROWS * m + ROWS)
+            z[t, 0, at] = jnp.where(even, faces[2 * m], faces[2 * m + 1])
+            z[t, 1, at] = jnp.where(even, faces[2 * m + 1], faces[2 * m])
 
     def put(t, x, j, k, new):
         if t < SWEEPS:
@@ -151,14 +157,13 @@
         held = [blank] * bands
         for x in range(nx) if planes is None else planes:
             for k in range(bands):
-                held[k] = packed(held[k], x, low(x, k), high(x, k))
+                held[k] = packed(held[k], x, k, low(x, k), high(x, k))
         return held
 
     for c in range(CHUNKS):
         wait(init_copies(c))
     face = packed_all(lambda x, k: v[0, x + 1, 0, rows(k)], lambda x, k: v[0, x + 1, tiles - 1, rows(k)])
-    for k in range(bands):
-        z[0, ROWS * k : ROWS * k + ROWS] = face[k]
+    ship(0, face)
 
     pl.semaphore_wait(barrier, 2 * len(AXES))
     start(z_copies(0) + x_copies(0) + y_copies(0))
@@ -225,48 +230,42 @@
     def mend(t, faces):
         for x in range(1, nx - 1):
             for k in range(bands):
-                value = turned(faces[k], -2 * x, 1)
+                value = turned(faces[k], -2 * x - k % 2, 1)
                 put_lane(t, x, 0, k, value, first_lane)
                 put_lane(t, x, tiles - 1, k, value, last_lane)
 
-    even = lane % 2 == 0
     edges = ((0, -1), (nx - 1, nx))
     for t in range(SWEEPS):
         wait(y_copies(t))
         bulk(t)
-        partial = packed_all(
-            lambda x, k: get(t + 1, x, 0, k), lambda x, k: get(t + 1, x, tiles - 1, k), range(1, nx - 1)
-        )
+        partial = packed_all(lambda x, k: get(t + 1, x, 0, k), lambda x, k: get(t + 1, x, tiles - 1, k))
         wait(x_copies(t) + z_copies(t))
-        planes = []
-        for x, outside in edges:
-            plane = [
-                [
-                    get(t + 1, x, j, k)
-                    + w[x, j, ROWS * k : ROWS * k + ROWS] * v[t, outside + 1, j, rows(k)]
-                    for k in range(bands)
-                ]
-                for j in range(tiles)
-            ]
-            for k in range(bands):
-                partial[k] = packed(partial[k], x, plane[0][k], plane[-1][k])
-            planes.append(plane)
+        from_low = [zh[t, 0, ROWS * m : ROWS * m + ROWS] for m in range(bands // 2)]
+        from_high = [zh[t, 1, ROWS * m : ROWS * m + ROWS] for m in range(bands // 2)]
+        halos = {x: [[v[t, outside + 1, j, rows(k)] for k in range(bands)] for j in range(tiles)] for x, outside in edges}
         faces = []
         for k in range(bands):
-            at = slice(ROWS * k, ROWS * k + ROWS)
-            halo = jnp.where(even, turned(zh[t, 0, at], 1, 1), turned(zh[t, 1, at], -1, 1))
-            faces.append(partial[k] + wz[k] * halo)
-            if t + 1 < SWEEPS:
-                z[t + 1, at] = faces[k]
+            low, high = turned(from_low[k // 2], 1, 1), turned(from_high[k // 2], -1, 1)
+            halo = jnp.where(even, low, high) if k % 2 == 0 else jnp.where(even, high, low)
+            outer = blank
+            for x, _ in edges:
+                outer = packed(outer, x, k, halos[x][0][k], halos[x][-1][k])
+            faces.append(partial[k] + wz[k] * (halo + outer))
         if t + 1 < SWEEPS:
+            ship(t + 1, faces)
             start(z_copies(t + 1))
-        for (x, _), plane in zip(edges, planes):
-            for k in range(bands):
-                value = turned(faces[k], -2 * x, 1)
-                plane[0][k] = jnp.where(first_lane, value, plane[0][k])
-                plane[-1][k] = jnp.where(last_lane, value, plane[-1][k])
+        for x, _ in edges:
+            for k in range(bands):
+                low = turned(from_low[k // 2], 1 - 2 * x - k % 2, 1)
+                high = turned(from_high[k // 2], -1 - 2 * x - k % 2, 1)
                 for j in range(tiles):
-                    put(t + 1, x, j, k, plane[j][k])
+                    halo = halos[x][j][k]
+                    if j == 0:
+                        halo = halo + jnp.where(first_lane, low, 0.0)
+                    if j == tiles - 1:
+                        halo = halo + jnp.where(last_lane, high, 0.0)
+                    new = get(t + 1, x, j, k) + w[x, j, ROWS * k : ROWS * k + ROWS] * halo
+                    put(t + 1, x, j, k, new)
         if t + 1 < SWEEPS:
             start(x_copies(t + 1))
         mend(t + 1, faces)
@@ -277,7 +276,7 @@
 def shards(initial, right_side, shift_field):
     nx, ny, nz = initial.shape
     assert nx % GROUP == 0 and nx % PREPARED == 0 and nx % CHUNKS == 0 and 2 * nx <= LANES
-    assert ny % ROWS == 0 and nz % LANES == 0
+    assert ny % (2 * ROWS) == 0 and nz % LANES == 0
     faces, tiles = 2 * len(AXES), nz // LANES
     return pl.pallas_call(
         kernel,
@@ -288,8 +287,8 @@
             pltpu.VMEM((SWEEPS, nx + 2, tiles, ny + 2 * ROWS, LANES), jnp.float32),
             pltpu.VMEM((nx, tiles, ny, LANES), jnp.float32),
             pltpu.VMEM((nx, tiles, ny, LANES), jnp.float32),
-            pltpu.VMEM((SWEEPS, ny, LANES), jnp.float32),
-            pltpu.VMEM((SWEEPS, 2, ny, LANES), jnp.float32),
+            pltpu.VMEM((SWEEPS, 2, ny // 2, LANES), jnp.float32),
+            pltpu.VMEM((SWEEPS, 2, ny // 2, LANES), jnp.float32),
             pltpu.SemaphoreType.DMA(((CHUNKS + 2) * tiles,)),
             pltpu.SemaphoreType.DMA((SWEEPS, faces)),
             pltpu.SemaphoreType.DMA((SWEEPS, faces)),

time: 23.2 us -> 22.8 us (0.983)
  Pallas kernels: 21.7 us -> 21.3 us
    pallas_call x1, Pallas kernels: 21.7 us -> 21.3 us  [shards(): pl.pallas_call(kernel, out_shape=pltpu.VMEM((nx, ny, nz), jnp.float32), i...]
where the time goes in v2:
time: 22.8 us; the launch traced here: 22.7 us
  Pallas kernels  21.3 us (93%)
  local copies, waits for them, and re-layouts  1.32 us (6%)
    pallas_call x1, Pallas kernels, shards(): pl.pallas_call(kernel, out_shape=pltpu.VMEM((nx, ny, nz), jnp.float32), i...  21.3 us
    unnamed x1, local copies, waits for them, and re-layouts  1.32 us

profile of v2, /device:TPU:0, one launch (start us, length us, event | category | flops | bytes accessed | tf_op | source)
XLA Modules:
  0.0 22.7 jit_solution(4418859550478038143)
XLA Ops:
  0.0 21.3 %shard_map.37 = f32[64,32,256]{2,1,0:T(8,128)S(1)} custom-call(f32[64,32,256]{2,1,0:T(8,128)} %init_ref.1, f32[64,32,256]{2,1,0:T(8,128)} %rhs_ref.1, f32[64,32,256]{2,1,0:T(8,128)} %shift_ref.1), custom_call_target="tpu_custom_call" | custom-call | tf_op jit(solution)/shard_map/pallas_call | solution.py:281
  21.3 1.3 %copy.5 = f32[64,32,256]{2,1,0:T(8,128)} copy(f32[64,32,256]{2,1,0:T(8,128)S(1)} %shard_map.37) | data formatting | bytes 4194304

commit v3 on v2

--- a/solution.py
+++ b/solution.py
@@ -9,13 +9,14 @@
 from jax.sharding import PartitionSpec as P
 
 SWEEPS = 4
+PAIR = SWEEPS - 2
 WEIGHT = np.float32(0.8)
 KEEP = np.float32(1.0) - WEIGHT
 AXES = ("gx", "gy", "gz")
 MESH = pl.DeviceIdType.MESH
 ROWS = 8
 LANES = 128
-GROUP = 16
+GROUP = 32
 PREPARED = 8
 CHUNKS = 4
 
@@ -23,6 +24,10 @@
 def beside(axis, step):
     count = lax.axis_size(axis)
     return {axis: lax.rem(lax.axis_index(axis) + (count + step), count)}
+
+
+def across(x_step, z_step):
+    return beside("gx", x_step) | beside("gz", z_step)
 
 
 def iota(dim, shape):
@@ -35,7 +40,9 @@
     return block if shift == 0 else pltpu.roll(block, shift, dim)
 
 
-def kernel(init_ref, rhs_ref, shift_ref, out_ref, v, q, w, z, zh, load, send, recv):
+def kernel(
+    init_ref, rhs_ref, shift_ref, out_ref, v, q, w, z, zh, zd, wh, u, uh, wz_out, wzh, uz, uzh, load, send, recv, send2, recv2
+):
     nx, ny, nz = out_ref.shape
     groups, bands, tiles = nx // GROUP, ny // ROWS, nz // LANES
     per = nx // CHUNKS
@@ -111,6 +118,44 @@
             remote(z.at[t, 0], zh.at[t, 1], t, 5, "gz", -1),
         )
 
+    def later(src, dst, slot, place):
+        return pltpu.make_async_remote_copy(
+            src_ref=src,
+            dst_ref=dst,
+            send_sem=send2.at[slot],
+            recv_sem=recv2.at[slot],
+            device_id=place,
+            device_id_type=MESH,
+        )
+
+    def weight_copies():
+        return (
+            later(w.at[nx - 1], wh.at[0], 0, beside("gx", 1)),
+            later(w.at[0], wh.at[1], 1, beside("gx", -1)),
+            later(wz_out.at[1], wzh.at[0], 2, beside("gz", 1)),
+            later(wz_out.at[0], wzh.at[1], 3, beside("gz", -1)),
+        )
+
+    def sum_x_copies():
+        return (
+            later(u.at[1], uh.at[0], 4, beside("gx", 1)),
+            later(u.at[0], uh.at[1], 5, beside("gx", -1)),
+        )
+
+    def sum_z_copies():
+        return (
+            later(uz.at[1], uzh.at[0], 6, beside("gz", 1)),
+            later(uz.at[0], uzh.at[1], 7, beside("gz", -1)),
+        )
+
+    def corner_copies():
+        return (
+            later(z.at[PAIR, 1], zd.at[0, 0], 8, across(1, 1)),
+            later(z.at[PAIR, 1], zd.at[0, 1], 9, across(-1, 1)),
+            later(z.at[PAIR, 0], zd.at[1, 0], 10, across(1, -1)),
+            later(z.at[PAIR, 0], zd.at[1, 1], 11, across(-1, -1)),
+        )
+
     lane = iota(1, (ROWS, LANES))
     first_lane = lane == 0
     last_lane = lane == LANES - 1
@@ -119,20 +164,17 @@
     def rows(k, shift=0):
         return slice(ROWS + ROWS * k + shift, 2 * ROWS + ROWS * k + shift)
 
-    def spots(x, k):
-        return (lane == (2 * x + k % 2) % LANES) | (lane == (2 * x + k % 2 - 1) % LANES)
-
-    def packed(held, x, k, low, high):
-        ends = jnp.where(first_lane, low, high)
-        return jnp.where(spots(x, k), turned(ends, 2 * x + k % 2, 1), held)
+    def packed(x, k, low, high):
+        ends = jnp.where(first_lane, low, jnp.where(last_lane, high, 0.0))
+        return turned(ends, 2 * x + k % 2, 1)
 
     even = lane % 2 == 0
 
-    def ship(t, faces):
+    def ship(held, faces):
         for m in range(bands // 2):
             at = slice(ROWS * m, ROWS * m + ROWS)
-            z[t, 0, at] = jnp.where(even, faces[2 * m], faces[2 * m + 1])
-            z[t, 1, at] = jnp.where(even, faces[2 * m + 1], faces[2 * m])
+            held[0, at] = jnp.where(even, faces[2 * m], faces[2 * m + 1])
+            held[1, at] = jnp.where(even, faces[2 * m + 1], faces[2 * m])
 
     def put(t, x, j, k, new):
         if t < SWEEPS:
@@ -153,17 +195,19 @@
                 out_ref.at[x, pl.ds(ROWS * k, ROWS), pl.ds(LANES * j, LANES)], new, mask=mask
             )
 
-    def packed_all(low, high, planes=None):
-        held = [blank] * bands
-        for x in range(nx) if planes is None else planes:
-            for k in range(bands):
-                held[k] = packed(held[k], x, k, low(x, k), high(x, k))
-        return held
+    def packed_all(low, high, ks):
+        faces = {}
+        for k in ks:
+            sums = [packed(x, k, low(x, k), high(x, k)) for x in range(nx)]
+            while len(sums) > 1:
+                sums = [a + b for a, b in zip(sums[0::2], sums[1::2])] + sums[len(sums) // 2 * 2 :]
+            faces[k] = sums[0]
+        return faces
 
     for c in range(CHUNKS):
         wait(init_copies(c))
-    face = packed_all(lambda x, k: v[0, x + 1, 0, rows(k)], lambda x, k: v[0, x + 1, tiles - 1, rows(k)])
-    ship(0, face)
+    face = packed_all(lambda x, k: v[0, x + 1, 0, rows(k)], lambda x, k: v[0, x + 1, tiles - 1, rows(k)], range(bands))
+    ship(z.at[0], face)
 
     pl.semaphore_wait(barrier, 2 * len(AXES))
     start(z_copies(0) + x_copies(0) + y_copies(0))
@@ -183,10 +227,14 @@
 
     lax.fori_loop(0, nx // PREPARED, prepare, 0)
     wz = packed_all(
-        lambda x, k: w[x, 0, ROWS * k : ROWS * k + ROWS], lambda x, k: w[x, tiles - 1, ROWS * k : ROWS * k + ROWS]
+        lambda x, k: w[x, 0, ROWS * k : ROWS * k + ROWS],
+        lambda x, k: w[x, tiles - 1, ROWS * k : ROWS * k + ROWS],
+        range(bands),
     )
-
-    def bulk_group(t, g, carry):
+    ship(wz_out, wz)
+    start(weight_copies())
+
+    def bulk_group(t, ks, g, carry):
         base = g * GROUP
         seen = {}
 
@@ -197,19 +245,19 @@
                     x = jnp.maximum(x, 0)
                 if i == GROUP:
                     x = jnp.minimum(x, nx - 1)
-                seen[i] = [[v[t, x + 1, j, rows(k)] for k in range(bands)] for j in range(tiles)]
+                seen[i] = [{k: v[t, x + 1, j, rows(k)] for k in ks} for j in range(tiles)]
                 if i < 0:
                     inside = jnp.where(g > 0, 1.0, 0.0)
-                    seen[i] = [[inside * cell for cell in column] for column in seen[i]]
+                    seen[i] = [{k: inside * column[k] for k in ks} for column in seen[i]]
                 if i == GROUP:
                     inside = jnp.where(g < groups - 1, 1.0, 0.0)
-                    seen[i] = [[inside * cell for cell in column] for column in seen[i]]
+                    seen[i] = [{k: inside * column[k] for k in ks} for column in seen[i]]
             return seen[i]
 
         for i in range(GROUP):
             x = base + i
             centre, below, above = plane(i), plane(i - 1), plane(i + 1)
-            for k in range(bands):
+            for k in ks:
                 at = slice(ROWS * k, ROWS * k + ROWS)
                 before = [turned(centre[j][k], 1, 1) for j in range(tiles)]
                 after = [turned(centre[j][k], -1, 1) for j in range(tiles)]
@@ -224,53 +272,117 @@
                     put(t + 1, x, j, k, (KEEP * centre[j][k] + q[x, j, at]) + w[x, j, at] * total)
         return carry
 
-    def bulk(t):
-        lax.fori_loop(0, groups, functools.partial(bulk_group, t), 0)
-
-    def mend(t, faces):
+    def bulk(t, ks):
+        lax.fori_loop(0, groups, functools.partial(bulk_group, t, ks), 0)
+
+    def mend(t, faces, ks):
         for x in range(1, nx - 1):
-            for k in range(bands):
+            for k in ks:
                 value = turned(faces[k], -2 * x - k % 2, 1)
                 put_lane(t, x, 0, k, value, first_lane)
                 put_lane(t, x, tiles - 1, k, value, last_lane)
 
     edges = ((0, -1), (nx - 1, nx))
+    inner, outer = tuple(range(1, bands - 1)), tuple(sorted({0, bands - 1}))
+
+    def halves(held):
+        return [held[ROWS * m : ROWS * m + ROWS] for m in range(bands // 2)]
+
+    def beyond(low, high, x):
+        cells = {}
+        for k in range(bands):
+            if tiles > 1:
+                for j in range(1, tiles - 1):
+                    cells[j, k] = 0.0
+            cells[0, k] = jnp.where(first_lane, turned(low[k // 2], 1 - 2 * x - k % 2, 1), 0.0)
+            last = jnp.where(last_lane, turned(high[k // 2], -1 - 2 * x - k % 2, 1), 0.0)
+            cells[tiles - 1, k] = last if tiles > 1 else cells[0, k] + last
+        return cells
+
+    def received(t):
+        halos = {
+            x: {(j, k): v[t, outside + 1, j, rows(k)] for j in range(tiles) for k in range(bands)} for x, outside in edges
+        }
+        return halos, halves(zh.at[t, 0]), halves(zh.at[t, 1])
+
+    def worked_out(t):
+        halos = {}
+        for side, (x, _) in enumerate(edges):
+            there = nx - 1 if side == 0 else 0
+            cells = beyond(halves(zd.at[0, side]), halves(zd.at[1, side]), there)
+            halos[x] = {}
+            for j in range(tiles):
+                for k in range(bands):
+                    at = slice(ROWS * k, ROWS * k + ROWS)
+                    total = v[t, x + 1, j, rows(k)] + cells[j, k]
+                    halos[x][j, k] = uh[side, j, at] + wh[side, j, at] * total
+        packs = []
+        for face in range(2):
+            turn = 1 if face else -1
+            own = halves(z.at[t, 1 if face else 0])
+            below, above = halves(zd.at[face, 0]), halves(zd.at[face, 1])
+            sums, weights = halves(uzh.at[face]), halves(wzh.at[face])
+            pack = []
+            for m in range(bands // 2):
+                total = turned(own[m], turn, 1)
+                start_lane = 0 if face else LANES - 1
+                at_first = (lane == start_lane) | (lane == (start_lane + 1) % LANES)
+                end_lane = (start_lane + 2 * (nx - 1)) % LANES
+                at_last = (lane == end_lane) | (lane == (end_lane + 1) % LANES)
+                total = total + jnp.where(at_first, turned(below[m], -2 * (nx - 1), 1), 0.0)
+                total = total + jnp.where(at_last, turned(above[m], 2 * (nx - 1), 1), 0.0)
+                pack.append(sums[m] + weights[m] * total)
+            packs.append(pack)
+        return halos, packs[0], packs[1]
+
     for t in range(SWEEPS):
+        def summed(ks):
+            bulk(t, ks)
+            return packed_all(lambda x, k: get(t + 1, x, 0, k), lambda x, k: get(t + 1, x, tiles - 1, k), ks)
+
+        partial = summed(inner) if inner else {}
         wait(y_copies(t))
-        bulk(t)
-        partial = packed_all(lambda x, k: get(t + 1, x, 0, k), lambda x, k: get(t + 1, x, tiles - 1, k))
-        wait(x_copies(t) + z_copies(t))
-        from_low = [zh[t, 0, ROWS * m : ROWS * m + ROWS] for m in range(bands // 2)]
-        from_high = [zh[t, 1, ROWS * m : ROWS * m + ROWS] for m in range(bands // 2)]
-        halos = {x: [[v[t, outside + 1, j, rows(k)] for k in range(bands)] for j in range(tiles)] for x, outside in edges}
+        partial |= summed(outer)
+        if t == PAIR:
+            for side, (x, _) in enumerate(edges):
+                for j in range(tiles):
+                    u[side, j] = v[t + 1, x + 1, j, ROWS : ROWS + ny]
+            start(sum_x_copies())
+        if t == PAIR:
+            ship(uz, partial)
+            start(sum_z_copies())
+        if t == PAIR + 1:
+            wait(sum_x_copies() + sum_z_copies() + corner_copies() + weight_copies())
+            halos, from_low, from_high = worked_out(PAIR)
+        else:
+            wait(x_copies(t) + z_copies(t))
+            halos, from_low, from_high = received(t)
+        sends = t + 1 < SWEEPS and t != PAIR
         faces = []
         for k in range(bands):
             low, high = turned(from_low[k // 2], 1, 1), turned(from_high[k // 2], -1, 1)
             halo = jnp.where(even, low, high) if k % 2 == 0 else jnp.where(even, high, low)
-            outer = blank
+            aside = blank
             for x, _ in edges:
-                outer = packed(outer, x, k, halos[x][0][k], halos[x][-1][k])
-            faces.append(partial[k] + wz[k] * (halo + outer))
-        if t + 1 < SWEEPS:
-            ship(t + 1, faces)
+                aside = aside + packed(x, k, halos[x][0, k], halos[x][tiles - 1, k])
+            faces.append(partial[k] + wz[k] * (halo + aside))
+        if sends:
+            ship(z.at[t + 1], faces)
             start(z_copies(t + 1))
+            if t + 1 == PAIR:
+                start(corner_copies())
         for x, _ in edges:
-            for k in range(bands):
-                low = turned(from_low[k // 2], 1 - 2 * x - k % 2, 1)
-                high = turned(from_high[k // 2], -1 - 2 * x - k % 2, 1)
-                for j in range(tiles):
-                    halo = halos[x][j][k]
-                    if j == 0:
-                        halo = halo + jnp.where(first_lane, low, 0.0)
-                    if j == tiles - 1:
-                        halo = halo + jnp.where(last_lane, high, 0.0)
-                    new = get(t + 1, x, j, k) + w[x, j, ROWS * k : ROWS * k + ROWS] * halo
+            cells = beyond(from_low, from_high, x)
+            for j in range(tiles):
+                for k in range(bands):
+                    new = get(t + 1, x, j, k) + w[x, j, ROWS * k : ROWS * k + ROWS] * (halos[x][j, k] + cells[j, k])
                     put(t + 1, x, j, k, new)
-        if t + 1 < SWEEPS:
+        if sends:
             start(x_copies(t + 1))
-        mend(t + 1, faces)
+        mend(t + 1, faces, outer)
         if t + 1 < SWEEPS:
             start(y_copies(t + 1))
+        mend(t + 1, faces, inner)
 
 
 def shards(initial, right_side, shift_field):
@@ -289,9 +401,19 @@
             pltpu.VMEM((nx, tiles, ny, LANES), jnp.float32),
             pltpu.VMEM((SWEEPS, 2, ny // 2, LANES), jnp.float32),
             pltpu.VMEM((SWEEPS, 2, ny // 2, LANES), jnp.float32),
+            pltpu.VMEM((2, 2, ny // 2, LANES), jnp.float32),
+            pltpu.VMEM((2, tiles, ny, LANES), jnp.float32),
+            pltpu.VMEM((2, tiles, ny, LANES), jnp.float32),
+            pltpu.VMEM((2, tiles, ny, LANES), jnp.float32),
+            pltpu.VMEM((2, ny // 2, LANES), jnp.float32),
+            pltpu.VMEM((2, ny // 2, LANES), jnp.float32),
+            pltpu.VMEM((2, ny // 2, LANES), jnp.float32),
+            pltpu.VMEM((2, ny // 2, LANES), jnp.float32),
             pltpu.SemaphoreType.DMA(((CHUNKS + 2) * tiles,)),
             pltpu.SemaphoreType.DMA((SWEEPS, faces)),
             pltpu.SemaphoreType.DMA((SWEEPS, faces)),
+            pltpu.SemaphoreType.DMA((12,)),
+            pltpu.SemaphoreType.DMA((12,)),
         ],
         compiler_params=pltpu.CompilerParams(
             collective_id=0, has_side_effects=True, vmem_limit_bytes=40 * 1024 * 1024

time: 22.8 us -> 22.2 us (0.974)
  Pallas kernels: 21.3 us -> 20.7 us
    pallas_call x1, Pallas kernels: 21.3 us -> 20.7 us  [shards(): pl.pallas_call(kernel, out_shape=pltpu.VMEM((nx, ny, nz), jnp.float32), i...]
where the time goes in v3:
time: 22.2 us; the launch traced here: 22 us
  Pallas kernels  20.7 us (93%)
  local copies, waits for them, and re-layouts  1.32 us (6%)
    pallas_call x1, Pallas kernels, shards(): pl.pallas_call(kernel, out_shape=pltpu.VMEM((nx, ny, nz), jnp.float32), i...  20.7 us
    unnamed x1, local copies, waits for them, and re-layouts  1.32 us

profile of v3, /device:TPU:0, one launch (start us, length us, event | category | flops | bytes accessed | tf_op | source)
XLA Modules:
  0.0 22.0 jit_solution(10537279754990783828)
XLA Ops:
  0.0 20.7 %shard_map.37 = f32[64,32,256]{2,1,0:T(8,128)S(1)} custom-call(f32[64,32,256]{2,1,0:T(8,128)} %init_ref.1, f32[64,32,256]{2,1,0:T(8,128)} %rhs_ref.1, f32[64,32,256]{2,1,0:T(8,128)} %shift_ref.1), custom_call_target="tpu_custom_call" | custom-call | tf_op jit(solution)/shard_map/pallas_call | solution.py:393
  20.7 1.3 %copy.5 = f32[64,32,256]{2,1,0:T(8,128)} copy(f32[64,32,256]{2,1,0:T(8,128)S(1)} %shard_map.37) | data formatting | bytes 4194304
